TPU v7x, 256 devices: a whole 4x4x8 slice. The times are simulated.
256 devices in a mesh: samples: 32 (over y, z), variants: 8 (over x, core).
Axes of the slice: x: 4, y: 4, z: 8, core: 2. Of those that a mesh axis runs over, the one named last changes fastest.
Arguments:
- genotypes: int32 [4096, 131072], P('variants', 'samples'), may hold values from 0 to 3, as said below
- weights: float32 [131072], P('samples'), may hold values from 0.25 to 20
Outputs:
- call_mean: float32 [4096], P('variants')
- call_var: float32 [4096], P('variants')
- class_counts: int32 [4, 4096], P(None, 'variants')
- ld_window: float32 [1024, 4096], P('samples', 'variants')
- sample_calls: int32 [2, 131072], P(None, 'samples')
- sample_share: float32 [131072], P('samples')
Inputs may be any that keep to these rules, and one draw needn't show every extreme that they name: `genotypes`: in every variant's row, each aligned group of 8 samples (samples 8 i to 8 i + 7) holds at least one call other than 3.
All inputs are finite; a program needn't handle non-finite values.
Results may differ from a plain program's by a relative error of at most 0.0004.
Values may be sent and summed in bfloat16 or wider, within the bound.
A program may use at most 64 MiB of HBM per device.

v0:
```python
import jax
import jax.numpy as jnp
from jax import lax
from jax.sharding import PartitionSpec as P


def sent_to_all(value, axis):
    size = lax.axis_size(axis)
    return lax.all_to_all(
        jnp.broadcast_to(value[None], (size, *value.shape)), axis, 0, 0, tiled=True
    )


def over_copies(value, axis):
    return sent_to_all(value, axis).sum(axis=0)


def in_one(arrays, axis):
    flat, at, outs = (jnp.concatenate([a.reshape(-1) for a in arrays]), 0, [])
    subtotal = over_copies(flat, axis)
    for a in arrays:
        outs.append(subtotal[at : at + a.size].reshape(a.shape))
        at += a.size
    return tuple(outs)


def shifted(value, axis, by):
    size = lax.axis_size(axis)
    pairs = [(i, i + by) for i in range(size) if 0 <= i + by < size]
    return lax.ppermute(value, axis, pairs)


def split_up(value, dim, size):
    before, after = (value.shape[:dim], value.shape[dim + 1 :])
    return jnp.moveaxis(value.reshape(*before, size, -1, *after), dim, 0)


def summed_on_arrival(value, axis, dim):
    size = lax.axis_size(axis)
    blocks = lax.all_to_all(split_up(value, dim, size), axis, 0, 0, tiled=True)
    return jnp.sum(blocks, axis=0)


def on_device(genotypes, weights):
    present = genotypes != 3
    called = present.astype(jnp.float32)
    dosage = jnp.where(present, genotypes, 0).astype(jnp.float32)
    weighted = called * weights[None, :]
    w_sum_part = jnp.sum(weighted, axis=1)
    first_part = jnp.sum(weighted * dosage, axis=1)
    classes = jnp.stack(
        [jnp.sum((genotypes == level).astype(jnp.float32), axis=1) for level in range(4)]
    )
    second_part = jnp.sum(weighted * dosage * dosage, axis=1)
    w_sum, first_total, second_total, class_total = in_one(
        (w_sum_part, first_part, second_part, classes), "samples"
    )
    mean_value = first_total / w_sum
    deviation = second_total - first_total * mean_value
    var_value = deviation / w_sum
    factor = 1.0 / jnp.sqrt(w_sum * (var_value + 1e-05))
    centered = (dosage - mean_value[:, None]) * called
    scaled = (jnp.sqrt(weights)[None, :] * centered * factor[:, None]).astype(jnp.bfloat16)
    following = shifted(scaled, "variants", -1)
    joined = jnp.concatenate([scaled, following], axis=0)
    ld_window = summed_on_arrival(
        lax.dot_general(
            joined, scaled, (((1,), (1,)), ((), ())), preferred_element_type=jnp.float32
        ),
        "samples",
        0,
    )
    squares = scaled.astype(jnp.float32)
    called_total, het_total, square_total = in_one(
        (
            jnp.sum(called, axis=0),
            jnp.sum((genotypes == 1).astype(jnp.float32), axis=0),
            jnp.sum(squares * squares, axis=0),
        ),
        "variants",
    )
    samples_all = weights.shape[0] * lax.axis_size("samples")
    variants_all = genotypes.shape[0] * lax.axis_size("variants")
    sample_share = square_total * (samples_all / variants_all)
    sample_calls = jnp.stack([called_total, het_total]).astype(jnp.int32)
    return (
        mean_value,
        var_value,
        class_total.astype(jnp.int32),
        ld_window,
        sample_calls,
        sample_share,
    )


def solution(mesh):
    placed = (P("variants", "samples"), P("samples"))
    return jax.shard_map(
        on_device,
        mesh=mesh,
        in_specs=placed,
        out_specs=(
            P("variants"),
            P("variants"),
            P(None, "variants"),
            P("samples", "variants"),
            P(None, "samples"),
            P("samples"),
        ),
        check_vma=False,
    )
```

profile of v0, /device:TPU:19, one launch (start us, length us, event | category | flops | bytes accessed | tf_op | source)
XLA Modules:
  0.0 165.1 jit_solution(6501759218654781641)
XLA Ops:
  0.6 0.0 copy-start
  0.6 0.0 copy-start.1
  0.7 5.0 %convert_reduce_fusion = (f32[4096]{0:T(1024)S(1)}, f32[512]{0:T(512)S(1)}) fusion(s32[512,4096]{1,0:T(8,128)} %param.2), kind=kLoop, calls=%fused_computation | loop fusion | flops 8384000 | bytes 8407040 | tf_op jit(solution)/shard_map/reduce_sum | solution.py:77
  5.7 0.7 copy-done
  6.4 0.0 copy-done.1
  6.4 6.4 %convert_reduce_fusion.2 = (f32[4096]{0:T(1024)S(1)}, f32[512]{0:T(512)S(1)}, f32[512]{0:T(512)S(1)}, f32[512]{0:T(512)S(1)}, f32[512]{0:T(512)S(1)}, /*index=5*/f32[512]{0:T(512)S(1)}, f32[512]{0:T(512)S(1)}) fusion(s32[512,4096]{1,0:T(8,128)S(1)} %copy-done, f32[4096]{0:T(1024)S(1)} %copy-done.1), kind=kLoop, calls=%fused_computation.12 | loop fusion | flops 41935872 | bytes 8433664 | tf_op jit(solution)/shard_map/reduce_sum | solution.py:76
  12.8 1.0 broadcast_in_dim.9
  13.8 11.0 %all-to-all-start = ((f32[32,1,3584]{2,1,0:T(1,128)}), f32[32,1,3584]{2,1,0:T(1,128)S(1)}, u32[]{:S(2)}, u32[]{:S(2)}) async-start(f32[32,1,3584]{2,1,0:T(1,128)} %broadcast_in_dim.9), calls=%async_computation | async-start | bytes 917504 | tf_op jit(solution)/shard_map/all_to_all | solution.py:9
  24.9 11.8 %all-to-all-done = f32[32,1,3584]{2,1,0:T(1,128)S(1)} async-done(((f32[32,1,3584]{2,1,0:T(1,128)}), f32[32,1,3584]{2,1,0:T(1,128)S(1)}, u32[]{:S(2)}, u32[]{:S(2)}) %all-to-all-start) | async-done | bytes 458784 | tf_op jit(solution)/shard_map/all_to_all | solution.py:9
  36.7 0.3 reduce_sum.124
  37.0 0.6 multiply_rsqrt_fusion
  37.6 0.0 copy-start.2
  37.6 6.4 %multiply_reduce_fusion = (f32[4096]{0:T(1024)S(1)}, bf16[512,4096]{1,0:T(8,128)(2,1)}) fusion(f32[512]{0:T(512)S(1)} %get-tuple-element.20, f32[512]{0:T(512)S(1)} %get-tuple-element.22, s32[512,4096]{1,0:T(8,128)} %param.2, f32[4096]{0:T(1024)S(1)} %sqrt.6), kind=kLoop, calls=%fused_computation.11 | loop fusion | flops 23064576 | bytes 12619776 | tf_op jit(solution)/shard_map/reduce_sum | solution.py:78
  44.0 5.4 %collective-permute-start = (bf16[512,4096]{1,0:T(8,128)(2,1)}, bf16[512,4096]{1,0:T(8,128)(2,1)}, u32[]{:S(2)}, u32[]{:S(2)}) collective-permute-start(bf16[512,4096]{1,0:T(8,128)(2,1)} %get-tuple-element.19), channel_id=1, source_target_pairs={{1,0},{2,1},{3,2},{4,3},{5,4},{6,5},{7,6},{9,8},{10,9},{11,10},{12... | collective-permute-start | bytes 12582920 | tf_op jit(solution)/shard_map/ppermute | solution.py:30
  49.4 1.0 broadcast_in_dim.10
  50.4 6.2 %all-to-all-start.2 = ((f32[8,1,12288]{2,1,0:T(1,128)}), f32[8,1,12288]{2,1,0:T(1,128)S(1)}, u32[]{:S(2)}, u32[]{:S(2)}) async-start(f32[8,1,12288]{2,1,0:T(1,128)} %broadcast_in_dim.10), calls=%async_computation.2 | async-start | bytes 786432 | tf_op jit(solution)/shard_map/all_to_all | solution.py:9
  56.6 42.5 %collective-permute-done = bf16[512,4096]{1,0:T(8,128)(2,1)} collective-permute-done((bf16[512,4096]{1,0:T(8,128)(2,1)}, bf16[512,4096]{1,0:T(8,128)(2,1)}, u32[]{:S(2)}, u32[]{:S(2)}) %collective-permute-start) | collective-permute-done | bytes 4194336 | tf_op jit(solution)/shard_map/ppermute | solution.py:30
  99.1 10.6 %fusion.3 = f32[1024,512]{1,0:T(8,128)} fusion(bf16[512,4096]{1,0:T(8,128)(2,1)} %get-tuple-element.19, bf16[512,4096]{1,0:T(8,128)(2,1)} %collective-permute-done), kind=kOutput, calls=%fused_computation.7 | convolution fusion | flops 4311744512 | bytes 10485760 | tf_op jit(solution)/shard_map/dot_general | solution.py:67
  109.7 0.0 copy-done.2
  109.7 0.0 all-to-all-done.2
  109.7 6.4 %all-to-all-start.1 = ((f32[32,32,512]{2,1,0:T(8,128)}), f32[32,32,512]{2,1,0:T(8,128)S(1)}, u32[]{:S(2)}, u32[]{:S(2)}) async-start(f32[32,32,512]{2,1,0:T(8,128)} %bitcast.11), calls=%async_computation.1 | async-start | bytes 4194304 | tf_op jit(solution)/shard_map/all_to_all | solution.py:40
  116.1 0.6 convert_element_type.40
  116.7 0.3 reduce_sum.129
  117.0 0.6 slice_multiply_fusion
  117.6 0.7 maximum_convert_fusion
  118.3 46.0 %all-to-all-done.1 = f32[32,32,512]{2,1,0:T(8,128)S(1)} async-done(((f32[32,32,512]{2,1,0:T(8,128)}), f32[32,32,512]{2,1,0:T(8,128)S(1)}, u32[]{:S(2)}, u32[]{:S(2)}) %all-to-all-start.1) | async-done | bytes 2097184 | tf_op jit(solution)/shard_map/all_to_all | solution.py:40
  164.3 0.8 reduce_sum.125
  (6 shorter events, 0.0 us)
Async XLA Ops:
  0.6 5.8 %copy-start = (s32[512,4096]{1,0:T(8,128)S(1)}, s32[512,4096]{1,0:T(8,128)}, u32[]{:S(2)}) copy-start(s32[512,4096]{1,0:T(8,128)} %param.2) | copy-start | bytes 25165828
  0.6 5.8 %copy-start.1 = (f32[4096]{0:T(1024)S(1)}, f32[4096]{0:T(1024)}, u32[]{:S(2)}) copy-start(f32[4096]{0:T(1024)} %param.3) | copy-start | bytes 49156
  13.8 22.9 %all-to-all-start = ((f32[32,1,3584]{2,1,0:T(1,128)}), f32[32,1,3584]{2,1,0:T(1,128)S(1)}, u32[]{:S(2)}, u32[]{:S(2)}) async-start(f32[32,1,3584]{2,1,0:T(1,128)} %broadcast_in_dim.9), calls=%async_computation | async-start | bytes 917504 | tf_op jit(solution)/shard_map/all_to_all | solution.py:9
  37.6 72.1 %copy-start.2 = (f32[512]{0:T(512)}, f32[512]{0:T(512)S(1)}, u32[]{:S(2)}) copy-start(f32[512]{0:T(512)S(1)} %get-tuple-element.22) | copy-start | bytes 6148
  44.0 55.1 %collective-permute-start = (bf16[512,4096]{1,0:T(8,128)(2,1)}, bf16[512,4096]{1,0:T(8,128)(2,1)}, u32[]{:S(2)}, u32[]{:S(2)}) collective-permute-start(bf16[512,4096]{1,0:T(8,128)(2,1)} %get-tuple-element.19), channel_id=1, source_target_pairs={{1,0},{2,1},{3,2},{4,3},{5,4},{6,5},{7,6},{9,8},{10,9},{11,10},{12... | collective-permute-start | bytes 12582920 | tf_op jit(solution)/shard_map/ppermute | solution.py:30
  50.4 59.3 %all-to-all-start.2 = ((f32[8,1,12288]{2,1,0:T(1,128)}), f32[8,1,12288]{2,1,0:T(1,128)S(1)}, u32[]{:S(2)}, u32[]{:S(2)}) async-start(f32[8,1,12288]{2,1,0:T(1,128)} %broadcast_in_dim.10), calls=%async_computation.2 | async-start | bytes 786432 | tf_op jit(solution)/shard_map/all_to_all | solution.py:9
  109.7 54.6 %all-to-all-start.1 = ((f32[32,32,512]{2,1,0:T(8,128)}), f32[32,32,512]{2,1,0:T(8,128)S(1)}, u32[]{:S(2)}, u32[]{:S(2)}) async-start(f32[32,32,512]{2,1,0:T(8,128)} %bitcast.11), calls=%async_computation.1 | async-start | bytes 4194304 | tf_op jit(solution)/shard_map/all_to_all | solution.py:40
where the time goes:
time: 167 us; the launch traced here: 165 us
  waiting for transfers between devices  100 us (60%)
  starting transfers between devices  29.1 us (17%)
  other arithmetic  21 us (13%)
  matrix products  10.6 us (6%)
  local copies, waits for them, and re-layouts  3.32 us (2%)
    all_to_all x1, waiting for transfers between devices, summed_on_arrival(): blocks = lax.all_to_all(split_up(value, dim, size), axis, 0, 0, tiled=True)  46 us
    ppermute x1, waiting for transfers between devices, shifted(): return lax.ppermute(value, axis, pairs)  42.5 us
    all_to_all x2, starting transfers between devices, sent_to_all(): lax.all_to_all(jnp.broadcast_to(value[None], (size, *value.shape)), axis,...  17.3 us
    all_to_all x2, waiting for transfers between devices, sent_to_all(): lax.all_to_all(jnp.broadcast_to(value[None], (size, *value.shape)), axis,...  11.8 us
    dot_general x1, matrix products, on_device(): lax.dot_general(joined, scaled, (((1,), (1,)), ((), ())), preferred_eleme...  10.6 us
    reduce_sum x1, other arithmetic, on_device(): jnp.sum(squares * squares, axis=0)  6.42 us
    all_to_all x1, starting transfers between devices, summed_on_arrival(): blocks = lax.all_to_all(split_up(value, dim, size), axis, 0, 0, tiled=True)  6.42 us
    reduce_sum x1, other arithmetic, on_device(): jnp.sum(called, axis=0)  6.37 us
  transfers between devices with their start and end apart: 4, of which 3 were waited for; matrix products, arithmetic and copies ran while one was open for 8% of the time, Pallas kernels for 0%

commit v1 on v0

v1 whole, which is shorter than its diff:
```python
import functools

import jax
import jax.numpy as jnp
from jax import lax
from jax.experimental import pallas as pl
from jax.experimental.pallas import tpu as pltpu
from jax.sharding import PartitionSpec as P

MESH = pl.DeviceIdType.MESH
LANES = 128
PARTS = 8
QUARTERS = 4
TILE = 16
HALF = jnp.float32
GAIN = 1.0
F32 = jnp.float32
NT = (((1,), (1,)), ((), ()))


def drain(ref, sem):
    pltpu.make_async_copy(ref, ref, sem).wait()


def folded(value):
    return sum(value[:, i : i + LANES] for i in range(0, value.shape[1], LANES))


def spread(value, width):
    return jnp.concatenate([value] * (width // LANES), axis=1)


def kernel(
    ny, nz, nv, samples_all,
    g_hbm, w_ref,
    mean_o, var_o, count_o, ld_o, calls_o, share_o,
    gbuf, raw, scl, recv_n, recv_p, wide_w, root_w, moments, codes, col, squares,
    crit_z, crit_y, cnt_z, cnt_y, mf, bcast, samp_s, samp_r, samp_g, acc,
    ysend, yrecv, zsend, zrecv, fin, fin_o, fin_n, fin_p,
    gsem, xs_n, xs_p, xr_n, xr_p, stat_s, stat_r, mf_s, mf_r, samp_ss, samp_rs,
    ys_sem, yr_sem, zs_sem, zr_sem, fo_s, fo_r, fn_s, fn_r, fp_s, fp_r,
):
    k, b = lax.axis_index("samples"), lax.axis_index("variants")
    y, z = k // nz, k % nz
    blocks = 4 * nz
    rows = blocks * TILE
    width = gbuf.shape[2] // PARTS
    half = PARTS // 2
    slice_w = gbuf.shape[2] // nv
    first, last = b == 0, b == nv - 1

    def at(ky, kz):
        return {"samples": ky * nz + kz}

    for part in range(8):
        group = pl.ds(part * (blocks // 8), blocks // 8)
        pltpu.make_async_copy(g_hbm.at[group], gbuf.at[group], gsem.at[part]).start()

    barrier = pltpu.get_barrier_semaphore()

    def greet(device):
        pl.semaphore_signal(barrier, inc=1, device_id=device, device_id_type=MESH)

    for d in range(1, ny):
        greet(at((y + d) % ny, z))
    for d in range(1, nz):
        greet(at(y, (z + d) % nz))
    for d in range(1, nv):
        greet({"variants": (b + d) % nv})

    @pl.when(b > 0)
    def _():
        for d in range(1, ny):
            greet({"samples": ((y + d) % ny) * nz + z, "variants": b - 1})

    @pl.when(b < nv - 1)
    def _():
        for d in range(1, ny):
            greet({"samples": ((y + d) % ny) * nz + z, "variants": b + 1})

    wide_w[...] = jnp.broadcast_to(w_ref[...], wide_w.shape)
    root_w[...] = jnp.sqrt(wide_w[...])
    col[...] = jnp.zeros_like(col)
    squares[...] = jnp.zeros_like(squares)

    def place(rb):
        return rb // (2 * nz), (rb // 2) % nz, rb % 2

    def first_pass(rb, carry):
        yr, zz, hh = place(rb)
        sum_w = jnp.zeros((TILE, LANES), F32)
        sum_1 = jnp.zeros((TILE, LANES), F32)
        sum_2 = jnp.zeros((TILE, LANES), F32)
        sum_c = jnp.zeros((TILE, LANES), jnp.int32)
        for kc in range(PARTS):
            cols = slice(kc * width, (kc + 1) * width)
            g = gbuf[rb, :, cols]
            gf = g.astype(F32)
            raw[kc, yr, zz, hh] = gf.astype(jnp.bfloat16)
            kept = jnp.where(g == 3, 0.0, wide_w[:, cols])
            once = kept * gf
            twice = once * gf
            code = jnp.left_shift(jnp.ones_like(g), g * 8)
            col[:, cols] += code[:8] + code[8:]
            sum_w += folded(kept)
            sum_1 += folded(once)
            sum_2 += folded(twice)
            sum_c += folded(code)
        moments[0, rb] = sum_w
        moments[1, rb] = sum_1
        moments[2, rb] = sum_2
        codes[rb] = sum_c
        return carry

    def copy_n(c):
        return pltpu.make_async_remote_copy(
            src_ref=raw.at[pl.ds(0, half), c // 2, :, c % 2],
            dst_ref=recv_n.at[c],
            send_sem=xs_n.at[c],
            recv_sem=xr_n.at[c],
            device_id={"variants": jnp.maximum(b - 1, 0)},
            device_id_type=MESH,
        )

    def copy_p(c):
        return pltpu.make_async_remote_copy(
            src_ref=raw.at[pl.ds(half, half), c // 2, pl.ds((c % 2) * (nz // 2), nz // 2)],
            dst_ref=recv_p.at[c],
            send_sem=xs_p.at[c],
            recv_sem=xr_p.at[c],
            device_id={"variants": jnp.minimum(b + 1, nv - 1)},
            device_id_type=MESH,
        )

    def wait_part(part):
        group = pl.ds(part * (blocks // 8), blocks // 8)
        pltpu.make_async_copy(g_hbm.at[group], gbuf.at[group], gsem.at[part]).wait()

    neighbours = jnp.where(b > 0, ny - 1, 0) + jnp.where(b < nv - 1, ny - 1, 0)
    for quarter in range(QUARTERS):
        for part in (2 * quarter, 2 * quarter + 1):
            wait_part(part)
            lax.fori_loop(part * (blocks // 8), (part + 1) * (blocks // 8), first_pass, 0)
        if quarter == 0:
            pl.semaphore_wait(barrier, (ny - 1) + (nz - 1) + (nv - 1) + neighbours)

        @pl.when(b < nv - 1)
        def _():
            copy_p(quarter).start()

        if quarter % 2 == 1:

            @pl.when(b > 0)
            def _():
                copy_n(quarter - 1).start()
                copy_n(quarter).start()

    def to_row(value):
        return jnp.sum(value.reshape(rows, LANES).T, axis=0, keepdims=True)

    def push(src, dst, i, device):
        return pltpu.make_async_remote_copy(
            src_ref=src,
            dst_ref=dst,
            send_sem=stat_s.at[i],
            recv_sem=stat_r.at[i],
            device_id=device,
            device_id_type=MESH,
        )

    for q in range(3):
        crit_z[z, q : q + 1, :] = to_row(moments[q])
    crit_z[z, 3:4, :] = jnp.zeros((1, rows), F32)
    for d in range(1, nz):
        push(crit_z.at[z], crit_z.at[z], 0, at(y, (z + d) % nz)).start()
    fields = codes[...]
    for level in range(4):
        field = jnp.bitwise_and(jnp.right_shift(fields, 8 * level), 255)
        cnt_z[z, level : level + 1, :] = to_row(field.astype(F32))
    for d in range(1, nz):
        push(cnt_z.at[z], cnt_z.at[z], 1, at(y, (z + d) % nz)).start()

    drain(crit_z.at[pl.ds(0, nz - 1)], stat_r.at[0])
    crit_y[y] = sum(crit_z[i] for i in range(nz))
    for d in range(1, ny):
        push(crit_y.at[y], crit_y.at[y], 2, at((y + d) % ny, z)).start()
    drain(cnt_z.at[pl.ds(0, nz - 1)], stat_r.at[1])
    cnt_y[y] = sum(cnt_z[i] for i in range(nz))
    for d in range(1, ny):
        push(cnt_y.at[y], cnt_y.at[y], 3, at((y + d) % ny, z)).start()
    drain(crit_y.at[pl.ds(0, ny - 1)], stat_r.at[2])
    total = sum(crit_y[i] for i in range(ny))
    w_sum, first_total, second_total = total[0:1], total[1:2], total[2:3]
    mean = first_total / w_sum
    var = (second_total - first_total * mean) / w_sum
    factor = 1.0 / jnp.sqrt(w_sum * (var + 1e-05))
    mean_o[...] = mean
    var_o[...] = var
    mf[0, 0:1, :] = mean
    mf[0, 1:2, :] = factor

    def mf_copy(slot, target):
        return pltpu.make_async_remote_copy(
            src_ref=mf.at[0],
            dst_ref=mf.at[slot],
            send_sem=mf_s.at[slot - 1],
            recv_sem=mf_r.at[slot - 1],
            device_id={"variants": target},
            device_id_type=MESH,
        )

    to_prev = mf_copy(1, jnp.maximum(b - 1, 0))
    to_next = mf_copy(2, jnp.minimum(b + 1, nv - 1))

    @pl.when(b > 0)
    def _():
        to_prev.start()

    @pl.when(b < nv - 1)
    def _():
        to_next.start()

    def widen(slot):
        for q in range(2):
            tall = jnp.broadcast_to(mf[slot, q : q + 1, :], (LANES, rows)).T
            bcast[slot, q] = tall.reshape(2, nz, 2, TILE, LANES)

    def scaled(value, roots, mean_rows, factor_rows):
        x = value.astype(F32)
        out = (roots * (x - spread(mean_rows, width))) * spread(factor_rows, width)
        return jnp.where(x > 2.5, 0.0, out).astype(jnp.bfloat16)

    widen(0)

    def second_pass(rb, carry):
        yr, zz, hh = place(rb)
        mean_rows, factor_rows = bcast[0, 0, yr, zz, hh], bcast[0, 1, yr, zz, hh]
        for kc in range(PARTS):
            cols = slice(kc * width, (kc + 1) * width)
            out = scaled(raw[kc, yr, zz, hh], root_w[:, cols], mean_rows, factor_rows)
            scl[kc, rb] = out
            wide = out.astype(F32)
            wide = wide * wide
            squares[:, cols] += wide[:8] + wide[8:]
        return carry

    lax.fori_loop(0, blocks, second_pass, 0)

    packed = col[...]
    missing = jnp.sum(jnp.bitwise_and(jnp.right_shift(packed, 24), 255), axis=0, keepdims=True)
    het = jnp.sum(jnp.bitwise_and(jnp.right_shift(packed, 8), 255), axis=0, keepdims=True)
    called = (rows - missing).astype(F32)
    het = het.astype(F32)
    share = jnp.sum(squares[...], axis=0, keepdims=True)
    for p in range(nv):
        cols = slice(p * slice_w, (p + 1) * slice_w)
        samp_s[p, 0:1, :] = called[:, cols]
        samp_s[p, 1:2, :] = het[:, cols]
        samp_s[p, 2:3, :] = share[:, cols]
        samp_s[p, 3:4, :] = jnp.zeros((1, slice_w), F32)
    samp_r[b] = samp_s[b]

    def samp_copy(i, src, dst, target):
        return pltpu.make_async_remote_copy(
            src_ref=src,
            dst_ref=dst,
            send_sem=samp_ss.at[i],
            recv_sem=samp_rs.at[i],
            device_id={"variants": target},
            device_id_type=MESH,
        )

    for d in range(1, nv):
        target = (b + d) % nv
        samp_copy(0, samp_s.at[target], samp_r.at[b], target).start()

    def y_copy(u, d):
        target = (y + d) % ny
        return pltpu.make_async_remote_copy(
            src_ref=ysend.at[u, target],
            dst_ref=yrecv.at[u, d - 1],
            send_sem=ys_sem.at[u],
            recv_sem=yr_sem.at[u],
            device_id=at(target, z),
            device_id_type=MESH,
        )

    def z_copy(u, d):
        target = (z + d) % nz
        return pltpu.make_async_remote_copy(
            src_ref=zsend.at[u, target],
            dst_ref=zrecv.at[u, d - 1],
            send_sem=zs_sem.at[u],
            recv_sem=zr_sem.at[u],
            device_id=at(y, target),
            device_id_type=MESH,
        )

    def y_start(u):
        for d in range(1, ny):
            y_copy(u, d).start()

    def y_fold(u):
        drain(yrecv.at[u], yr_sem.at[u])
        part = ysend[u, y].astype(F32)
        for d in range(ny - 1):
            part = part + yrecv[u, d].astype(F32)
        zsend[u] = part.astype(HALF)
        for d in range(1, nz):
            z_copy(u, d).start()

    def z_fold(u):
        drain(zrecv.at[u], zr_sem.at[u])
        part = zsend[u, z].astype(F32)
        for d in range(nz - 1):
            part = part + zrecv[u, d].astype(F32)
        fin[u] = part * (1.0 / GAIN)

    qw = rows // QUARTERS

    def group_rows(value, u):
        value = (value * GAIN).astype(HALF).reshape(2, nz, 2, TILE, qw)
        for yr in range(2):
            for hh in range(2):
                ysend[u, 2 * yr + hh] = value[yr, :, hh]

    for pair in range(2):
        acc[...] = jnp.zeros_like(acc)

        def own(kc, carry):
            left = scl[kc].reshape(rows, width)
            right = scl[kc, pair * (blocks // 2) : (pair + 1) * (blocks // 2)]
            acc[...] += lax.dot_general(
                left, right.reshape(rows // 2, width), NT, preferred_element_type=F32
            )
            return carry

        lax.fori_loop(0, PARTS, own, 0)
        for j in range(2):
            group_rows(acc[:, j * qw : (j + 1) * qw], 2 * pair + j)
            y_start(2 * pair + j)

    @pl.when(b < nv - 1)
    def _():
        to_prev.wait_recv()
        widen(1)

    @pl.when(b > 0)
    def _():
        to_next.wait_recv()
        widen(2)

    def chunk_n(c):
        copy_n(c).wait_recv()
        for kc in range(half):
            roots = root_w[:, kc * width : (kc + 1) * width]
            for zz in range(nz):
                recv_n[c, kc, zz] = scaled(
                    recv_n[c, kc, zz],
                    roots,
                    bcast[1, 0, c // 2, zz, c % 2],
                    bcast[1, 1, c // 2, zz, c % 2],
                )
        out = jnp.zeros((nz * TILE, rows), F32)
        for kc in range(half):
            out = out + lax.dot_general(
                recv_n[c, kc].reshape(nz * TILE, width),
                scl[kc].reshape(rows, width),
                NT,
                preferred_element_type=F32,
            )
        out = (out * GAIN).astype(HALF)
        for q in range(QUARTERS):
            ysend[4 + c, q] = out[:, q * qw : (q + 1) * qw].reshape(nz, TILE, qw)
        y_start(4 + c)

    def chunk_p(c):
        copy_p(c).wait_recv()
        for kc in range(half):
            roots = root_w[:, (half + kc) * width : (half + kc + 1) * width]
            for zz in range(nz // 2):
                for hh in range(2):
                    spot = (c // 2, (c % 2) * (nz // 2) + zz, hh)
                    recv_p[c, kc, zz, hh] = scaled(
                        recv_p[c, kc, zz, hh], roots, bcast[(2, 0, *spot)], bcast[(2, 1, *spot)]
                    )
        out = jnp.zeros((rows, qw), F32)
        for kc in range(half):
            out = out + lax.dot_general(
                scl[half + kc].reshape(rows, width),
                recv_p[c, kc].reshape(qw, width),
                NT,
                preferred_element_type=F32,
            )
        group_rows(out, 8 + c)
        y_start(8 + c)

    def n_copy(c):
        return pltpu.make_async_remote_copy(
            src_ref=fin.at[4 + c],
            dst_ref=fin_n.at[c % 2, y],
            send_sem=fn_s.at[c],
            recv_sem=fn_r.at[c % 2],
            device_id=at(2 + c // 2, z),
            device_id_type=MESH,
        )

    def o_copy():
        return pltpu.make_async_remote_copy(
            src_ref=fin.at[pl.ds(0, QUARTERS)],
            dst_ref=fin_o.at[y % 2],
            send_sem=fo_s.at[0],
            recv_sem=fo_r.at[y % 2],
            device_id=at(y // 2, z),
            device_id_type=MESH,
        )

    def p_copy():
        return pltpu.make_async_remote_copy(
            src_ref=fin.at[pl.ds(8, QUARTERS)],
            dst_ref=fin_p.at[y % 2],
            send_sem=fp_s.at[0],
            recv_sem=fp_r.at[y % 2],
            device_id={"samples": (2 + y // 2) * nz + z, "variants": jnp.maximum(b - 1, 0)},
            device_id_type=MESH,
        )

    def n_final(c):
        owner = 2 + c // 2

        @pl.when(y == owner)
        def _():
            fin_n[c % 2, y] = fin[4 + c]

        @pl.when(y != owner)
        def _():
            n_copy(c).start()

    def step(c, carry):
        @pl.when(c < QUARTERS)
        def _():
            @pl.when(b < nv - 1)
            def _():
                chunk_n(c)

            @pl.when(b > 0)
            def _():
                chunk_p(c)

        @pl.when(c == 0)
        def _():
            for u in range(QUARTERS):
                y_fold(u)

        @pl.when((c >= 1) & (c <= QUARTERS))
        def _():
            @pl.when(b < nv - 1)
            def _():
                y_fold(4 + c - 1)

            @pl.when(b > 0)
            def _():
                y_fold(8 + c - 1)

        @pl.when(c == 1)
        def _():
            for u in range(QUARTERS):
                z_fold(u)

            @pl.when(y == 0)
            def _():
                fin_o[0] = fin[0:QUARTERS]

            @pl.when(y > 0)
            def _():
                o_copy().start()

            drain(samp_r.at[pl.ds(0, nv - 1)], samp_rs.at[0])
            samp_g[b] = sum(samp_r[p] for p in range(nv))
            for d in range(1, nv):
                samp_copy(1, samp_g.at[b], samp_g.at[b], (b + d) % nv).start()

        @pl.when(c >= 2)
        def _():
            @pl.when(b < nv - 1)
            def _():
                z_fold(4 + c - 2)
                n_final(c - 2)

            @pl.when(b > 0)
            def _():
                z_fold(8 + c - 2)

        return carry

    lax.fori_loop(0, QUARTERS + 2, step, 0)

    @pl.when(b > 0)
    def _():
        p_copy().start()

    drain(cnt_y.at[pl.ds(0, ny - 1)], stat_r.at[3])
    count_o[...] = sum(cnt_y[i] for i in range(ny)).astype(jnp.int32)
    drain(samp_g.at[pl.ds(0, nv - 1)], samp_rs.at[1])
    for p in range(nv):
        cols = slice(p * slice_w, (p + 1) * slice_w)
        calls_o[:, cols] = samp_g[p, 0:2, :].astype(jnp.int32)
        share_o[:, cols] = samp_g[p, 2:3, :] * (samples_all / (nv * rows))

    @pl.when(y == 0)
    def _():
        drain(fin_o.at[1], fo_r.at[1])

    @pl.when(y == 1)
    def _():
        drain(fin_o.at[0], fo_r.at[0])
        drain(fin_o.at[1], fo_r.at[1])

    @pl.when(y < 2)
    def _():
        for h in range(2):
            for q in range(QUARTERS):
                ld_o[h * TILE : (h + 1) * TILE, q * qw : (q + 1) * qw] = fin_o[h, q]

    @pl.when(y >= 2)
    def _():
        @pl.when(b < nv - 1)
        def _():
            for h in range(2):
                drain(fin_n.at[h, pl.ds(0, ny - 1)], fn_r.at[h])
                drain(fin_p.at[h], fp_r.at[h])
            for h in range(2):
                for q in range(QUARTERS):
                    ld_o[h * TILE : (h + 1) * TILE, q * qw : (q + 1) * qw] = (
                        fin_n[h, q] + fin_p[h, q]
                    )

        @pl.when(b == nv - 1)
        def _():
            ld_o[...] = jnp.zeros_like(ld_o)

    drain(crit_z.at[pl.ds(0, nz - 1)], stat_s.at[0])
    drain(cnt_z.at[pl.ds(0, nz - 1)], stat_s.at[1])
    drain(crit_y.at[pl.ds(0, ny - 1)], stat_s.at[2])
    drain(cnt_y.at[pl.ds(0, ny - 1)], stat_s.at[3])
    drain(samp_r.at[pl.ds(0, nv - 1)], samp_ss.at[0])
    drain(samp_g.at[pl.ds(0, nv - 1)], samp_ss.at[1])

    def sent(u, carry):
        drain(yrecv.at[u], ys_sem.at[u])
        drain(zrecv.at[u], zs_sem.at[u])
        return carry

    lax.fori_loop(0, QUARTERS, sent, 0)

    @pl.when(y > 0)
    def _():
        o_copy().wait_send()

    @pl.when(b < nv - 1)
    def _():
        lax.fori_loop(QUARTERS, 2 * QUARTERS, sent, 0)
        to_next.wait_send()
        for c in range(QUARTERS):
            copy_p(c).wait_send()

            @pl.when(y != 2 + c // 2)
            def _():
                n_copy(c).wait_send()

    @pl.when(b > 0)
    def _():
        lax.fori_loop(2 * QUARTERS, 3 * QUARTERS, sent, 0)
        to_prev.wait_send()
        p_copy().wait_send()
        for c in range(QUARTERS):
            copy_n(c).wait_send()


def on_device(ny, nz, nv, genotypes, weights):
    rows, cols = genotypes.shape
    blocks = rows // TILE
    width, qw, slice_w = cols // PARTS, rows // QUARTERS, cols // nv
    half = PARTS // 2
    bf16 = jnp.bfloat16
    vmem = pl.BlockSpec(memory_space=pltpu.VMEM)
    dma = pltpu.SemaphoreType.DMA
    units = 3 * QUARTERS
    shapes = (
        ((1, rows), F32),
        ((1, rows), F32),
        ((4, rows), jnp.int32),
        ((2 * TILE, rows), F32),
        ((2, cols), jnp.int32),
        ((1, cols), F32),
    )
    mean, var, counts, ld, calls, share = pl.pallas_call(
        functools.partial(kernel, ny, nz, nv, cols * ny * nz),
        out_shape=[jax.ShapeDtypeStruct(s, t) for s, t in shapes],
        in_specs=[pl.BlockSpec(memory_space=pl.ANY), vmem],
        out_specs=[vmem] * len(shapes),
        scratch_shapes=[
            pltpu.VMEM((blocks, TILE, cols), jnp.int32),
            pltpu.VMEM((PARTS, 2, nz, 2, TILE, width), bf16),
            pltpu.VMEM((PARTS, blocks, TILE, width), bf16),
            pltpu.VMEM((QUARTERS, half, nz, TILE, width), bf16),
            pltpu.VMEM((QUARTERS, half, nz // 2, 2, TILE, width), bf16),
            pltpu.VMEM((TILE, cols), F32),
            pltpu.VMEM((TILE, cols), F32),
            pltpu.VMEM((3, blocks, TILE, LANES), F32),
            pltpu.VMEM((blocks, TILE, LANES), jnp.int32),
            pltpu.VMEM((8, cols), jnp.int32),
            pltpu.VMEM((8, cols), F32),
            pltpu.VMEM((nz, 4, rows), F32),
            pltpu.VMEM((ny, 4, rows), F32),
            pltpu.VMEM((nz, 4, rows), F32),
            pltpu.VMEM((ny, 4, rows), F32),
            pltpu.VMEM((3, 2, rows), F32),
            pltpu.VMEM((3, 2, 2, nz, 2, TILE, LANES), F32),
            pltpu.VMEM((nv, 4, slice_w), F32),
            pltpu.VMEM((nv, 4, slice_w), F32),
            pltpu.VMEM((nv, 4, slice_w), F32),
            pltpu.VMEM((rows, rows // 2), F32),
            pltpu.VMEM((units, ny, nz, TILE, qw), HALF),
            pltpu.VMEM((units, ny - 1, nz, TILE, qw), HALF),
            pltpu.VMEM((units, nz, TILE, qw), HALF),
            pltpu.VMEM((units, nz - 1, TILE, qw), HALF),
            pltpu.VMEM((units, TILE, qw), F32),
            pltpu.VMEM((2, QUARTERS, TILE, qw), F32),
            pltpu.VMEM((2, QUARTERS, TILE, qw), F32),
            pltpu.VMEM((2, QUARTERS, TILE, qw), F32),
            dma((8,)),
            dma((QUARTERS,)),
            dma((QUARTERS,)),
            dma((QUARTERS,)),
            dma((QUARTERS,)),
            dma((4,)),
            dma((4,)),
            dma((2,)),
            dma((2,)),
            dma((2,)),
            dma((2,)),
            dma((units,)),
            dma((units,)),
            dma((units,)),
            dma((units,)),
            dma((1,)),
            dma((2,)),
            dma((QUARTERS,)),
            dma((2,)),
            dma((1,)),
            dma((2,)),
        ],
        compiler_params=pltpu.CompilerParams(
            collective_id=0, has_side_effects=True, vmem_limit_bytes=60 * 2**20
        ),
    )(genotypes.reshape(blocks, TILE, cols), weights.reshape(1, cols))
    return (
        mean.reshape(rows),
        var.reshape(rows),
        counts,
        ld,
        calls,
        share.reshape(cols),
    )


def solution(mesh):
    ny = 4
    return jax.shard_map(
        functools.partial(on_device, ny, mesh.shape["samples"] // ny, mesh.shape["variants"]),
        mesh=mesh,
        in_specs=(P("variants", "samples"), P("samples")),
        out_specs=(
            P("variants"),
            P("variants"),
            P(None, "variants"),
            P("samples", "variants"),
            P(None, "samples"),
            P("samples"),
        ),
        check_vma=False,
    )
```

time: 167 us -> 80.8 us (0.48)
  waiting for transfers between devices: 100 us -> 0 us
  Pallas kernels: 0 us -> 71.6 us
  starting transfers between devices: 29.1 us -> 0 us
  other arithmetic: 21 us -> 0 us
  matrix products: 10.6 us -> 0 us
  local copies, waits for them, and re-layouts: 3.32 us -> 7.96 us
    pallas_call x0 -> x1, Pallas kernels: none -> 71.6 us  [on_device(): pl.pallas_call(functools.partial(kernel, ny, nz, nv, cols * ny * nz), out...]
    all_to_all x3 -> x0, waiting for transfers between devices: 57.9 us -> none  [the longest x1 46 us: summed_on_arrival(): blocks = lax.all_to_all(split_up(value, dim, size), axis, 0, 0, tiled=True)]
    ppermute x1 -> x0, waiting for transfers between devices: 42.5 us -> none  [shifted(): return lax.ppermute(value, axis, pairs)]
    all_to_all x3 -> x0, starting transfers between devices: 23.7 us -> none  [the longest x2 17.3 us: sent_to_all(): lax.all_to_all(jnp.broadcast_to(value[None], (size, *value.shape)), axis,...]
    reduce_sum x6 -> x0, other arithmetic: 19.2 us -> none  [the longest x1 6.42 us: on_device(): jnp.sum(squares * squares, axis=0)]
    dot_general x1 -> x0, matrix products: 10.6 us -> none  [on_device(): lax.dot_general(joined, scaled, (((1,), (1,)), ((), ())), preferred_eleme...]
    unnamed x7 -> x6, local copies, waits for them, and re-layouts: 0.72 us -> 7.96 us
    ppermute x1 -> x0, starting transfers between devices: 5.37 us -> none  [shifted(): return lax.ppermute(value, axis, pairs)]
  transfers between devices with their start and end apart: 4 -> 0, of which waited for: 3 -> 0; matrix products, arithmetic and copies ran while one was open for 8% -> 0% of each run, Pallas kernels for 0% -> 0%
where the time goes in v1:
time: 80.8 us; the launch traced here: 80.2 us
  Pallas kernels  71.6 us (89%)
  local copies, waits for them, and re-layouts  7.96 us (10%)
    pallas_call x1, Pallas kernels, on_device(): pl.pallas_call(functools.partial(kernel, ny, nz, nv, cols * ny * nz), out...  71.6 us
    unnamed x6, local copies, waits for them, and re-layouts  7.96 us

profile of v1, /device:TPU:19, one launch (start us, length us, event | category | flops | bytes accessed | tf_op | source)
XLA Modules:
  0.0 80.2 jit_solution(11119444474814436679)
XLA Ops:
  0.6 71.6 %shard_map.73 = (f32[1,512]{1,0:T(1,128)}, f32[1,512]{1,0:T(1,128)}, s32[4,512]{1,0:T(4,128)}, f32[32,512]{1,0:T(8,128)}, s32[2,4096]{1,0:T(2,128)}, /*index=5*/f32[1,4096]{1,0:T(1,128)}) custom-call(s32[32,16,4096]{2,1,0:T(8,128)} %bitcast.5, f32[1,4096]{1,0:T(1,128)} %bitcast.6), custom_call_target="tpu_custom_call" | custom-call | tf_op jit(solution)/shard_map/pallas_call | solution.py:597
  72.2 1.3 %copy.14 = f32[512]{0:T(512)} copy(f32[512]{0:T(512)} %bitcast.9) | data formatting | bytes 4096
  73.5 1.2 %copy.15 = f32[512]{0:T(512)} copy(f32[512]{0:T(512)} %bitcast.8) | data formatting | bytes 4096
  74.7 1.3 %copy.16 = s32[4,512]{1,0:T(4,128)} copy(s32[4,512]{1,0:T(4,128)} %get-tuple-element.26) | data formatting | bytes 16384
  76.0 1.5 %copy.17 = f32[32,512]{1,0:T(8,128)} copy(f32[32,512]{1,0:T(8,128)} %get-tuple-element.27) | data formatting | bytes 131072
  77.5 1.4 %copy.18 = s32[2,4096]{1,0:T(2,128)} copy(s32[2,4096]{1,0:T(2,128)} %get-tuple-element.28) | data formatting | bytes 65536
  78.9 1.3 %copy.19 = f32[4096]{0:T(1024)} copy(f32[4096]{0:T(1024)} %bitcast.7) | data formatting | bytes 32768

commit v2 on v1

--- a/solution.py
+++ b/solution.py
@@ -12,8 +12,8 @@
 PARTS = 8
 QUARTERS = 4
 TILE = 16
-HALF = jnp.float32
-GAIN = 1.0
+HALF = jnp.int16
+STEPS = 32000.0
 F32 = jnp.float32
 NT = (((1,), (1,)), ((), ()))
 
@@ -26,19 +26,29 @@
     return sum(value[:, i : i + LANES] for i in range(0, value.shape[1], LANES))
 
 
+def coded(value):
+    size = jnp.minimum(jnp.sqrt(jnp.abs(value)) * STEPS + 0.5, 32767.0).astype(jnp.int32)
+    return jnp.where(value < 0.0, -size, size).astype(HALF)
+
+
+def decoded(code):
+    value = code.astype(jnp.int32).astype(F32)
+    return value * jnp.abs(value)
+
+
 def spread(value, width):
     return jnp.concatenate([value] * (width // LANES), axis=1)
 
 
 def kernel(
-    ny, nz, nv, samples_all,
+    ny, nz, nv,
     g_hbm, w_ref,
-    mean_o, var_o, count_o, ld_o, calls_o, share_o,
-    gbuf, raw, scl, recv_n, recv_p, wide_w, root_w, moments, codes, col, squares,
+    stat_o, ld_o, samp_o,
+    gbuf, raw, scl, scl_n, scl_p, recv_n, recv_p, wide_w, root_w, moments, codes, col, squares,
     crit_z, crit_y, cnt_z, cnt_y, mf, bcast, samp_s, samp_r, samp_g, acc,
-    ysend, yrecv, zsend, zrecv, fin, fin_o, fin_n, fin_p,
+    ysend, yfar, ynear, zsend, zrecv, fin, fin_o, fin_n, fin_p,
     gsem, xs_n, xs_p, xr_n, xr_p, stat_s, stat_r, mf_s, mf_r, samp_ss, samp_rs,
-    ys_sem, yr_sem, zs_sem, zr_sem, fo_s, fo_r, fn_s, fn_r, fp_s, fp_r,
+    ya_s, ya_r, yb_s, yb_r, zs_sem, zr_sem, fo_s, fo_r, fn_s, fn_r, fp_s, fp_r,
 ):
     k, b = lax.axis_index("samples"), lax.axis_index("variants")
     y, z = k // nz, k % nz
@@ -91,7 +101,6 @@
         sum_w = jnp.zeros((TILE, LANES), F32)
         sum_1 = jnp.zeros((TILE, LANES), F32)
         sum_2 = jnp.zeros((TILE, LANES), F32)
-        sum_c = jnp.zeros((TILE, LANES), jnp.int32)
         for kc in range(PARTS):
             cols = slice(kc * width, (kc + 1) * width)
             g = gbuf[rb, :, cols]
@@ -100,15 +109,22 @@
             kept = jnp.where(g == 3, 0.0, wide_w[:, cols])
             once = kept * gf
             twice = once * gf
-            code = jnp.left_shift(jnp.ones_like(g), g * 8)
-            col[:, cols] += code[:8] + code[8:]
             sum_w += folded(kept)
             sum_1 += folded(once)
             sum_2 += folded(twice)
-            sum_c += folded(code)
         moments[0, rb] = sum_w
         moments[1, rb] = sum_1
         moments[2, rb] = sum_2
+        return carry
+
+    def count_pass(rb, carry):
+        sum_c = jnp.zeros((TILE, LANES), jnp.int32)
+        for kc in range(PARTS):
+            cols = slice(kc * width, (kc + 1) * width)
+            g = gbuf[rb, :, cols]
+            code = jnp.left_shift(jnp.ones_like(g), g * 8)
+            col[:, cols] += code[:8] + code[8:]
+            sum_c += folded(code)
         codes[rb] = sum_c
         return carry
 
@@ -137,23 +153,18 @@
         pltpu.make_async_copy(g_hbm.at[group], gbuf.at[group], gsem.at[part]).wait()
 
     neighbours = jnp.where(b > 0, ny - 1, 0) + jnp.where(b < nv - 1, ny - 1, 0)
-    for quarter in range(QUARTERS):
-        for part in (2 * quarter, 2 * quarter + 1):
-            wait_part(part)
-            lax.fori_loop(part * (blocks // 8), (part + 1) * (blocks // 8), first_pass, 0)
-        if quarter == 0:
-            pl.semaphore_wait(barrier, (ny - 1) + (nz - 1) + (nv - 1) + neighbours)
-
+    for part in range(8):
+        wait_part(part)
+        lax.fori_loop(part * (blocks // 8), (part + 1) * (blocks // 8), first_pass, 0)
+
+    def start_chunk(c):
         @pl.when(b < nv - 1)
         def _():
-            copy_p(quarter).start()
-
-        if quarter % 2 == 1:
-
-            @pl.when(b > 0)
-            def _():
-                copy_n(quarter - 1).start()
-                copy_n(quarter).start()
+            copy_p(c).start()
+
+        @pl.when(b > 0)
+        def _():
+            copy_n(c).start()
 
     def to_row(value):
         return jnp.sum(value.reshape(rows, LANES).T, axis=0, keepdims=True)
@@ -171,8 +182,12 @@
     for q in range(3):
         crit_z[z, q : q + 1, :] = to_row(moments[q])
     crit_z[z, 3:4, :] = jnp.zeros((1, rows), F32)
+    pl.semaphore_wait(barrier, (ny - 1) + (nz - 1) + (nv - 1) + neighbours)
     for d in range(1, nz):
         push(crit_z.at[z], crit_z.at[z], 0, at(y, (z + d) % nz)).start()
+    start_chunk(0)
+    start_chunk(1)
+    lax.fori_loop(0, blocks, count_pass, 0)
     fields = codes[...]
     for level in range(4):
         field = jnp.bitwise_and(jnp.right_shift(fields, 8 * level), 255)
@@ -184,18 +199,16 @@
     crit_y[y] = sum(crit_z[i] for i in range(nz))
     for d in range(1, ny):
         push(crit_y.at[y], crit_y.at[y], 2, at((y + d) % ny, z)).start()
-    drain(cnt_z.at[pl.ds(0, nz - 1)], stat_r.at[1])
-    cnt_y[y] = sum(cnt_z[i] for i in range(nz))
-    for d in range(1, ny):
-        push(cnt_y.at[y], cnt_y.at[y], 3, at((y + d) % ny, z)).start()
+    start_chunk(2)
     drain(crit_y.at[pl.ds(0, ny - 1)], stat_r.at[2])
     total = sum(crit_y[i] for i in range(ny))
     w_sum, first_total, second_total = total[0:1], total[1:2], total[2:3]
     mean = first_total / w_sum
     var = (second_total - first_total * mean) / w_sum
     factor = 1.0 / jnp.sqrt(w_sum * (var + 1e-05))
-    mean_o[...] = mean
-    var_o[...] = var
+    stat_o[0:1, :] = mean
+    stat_o[1:2, :] = var
+    stat_o[2:4, :] = jnp.zeros((2, rows), F32)
     mf[0, 0:1, :] = mean
     mf[0, 1:2, :] = factor
 
@@ -220,6 +233,8 @@
     def _():
         to_next.start()
 
+    start_chunk(3)
+
     def widen(slot):
         for q in range(2):
             tall = jnp.broadcast_to(mf[slot, q : q + 1, :], (LANES, rows)).T
@@ -231,6 +246,11 @@
         return jnp.where(x > 2.5, 0.0, out).astype(jnp.bfloat16)
 
     widen(0)
+
+    drain(cnt_z.at[pl.ds(0, nz - 1)], stat_r.at[1])
+    cnt_y[y] = sum(cnt_z[i] for i in range(nz))
+    for d in range(1, ny):
+        push(cnt_y.at[y], cnt_y.at[y], 3, at((y + d) % ny, z)).start()
 
     def second_pass(rb, carry):
         yr, zz, hh = place(rb)
@@ -238,27 +258,18 @@
         for kc in range(PARTS):
             cols = slice(kc * width, (kc + 1) * width)
             out = scaled(raw[kc, yr, zz, hh], root_w[:, cols], mean_rows, factor_rows)
-            scl[kc, rb] = out
-            wide = out.astype(F32)
+            scl[pl.ds(pl.multiple_of(rb * TILE, TILE), TILE), cols] = out
+        return carry
+
+    def square_pass(rb, carry):
+        for kc in range(PARTS):
+            cols = slice(kc * width, (kc + 1) * width)
+            wide = scl[pl.ds(pl.multiple_of(rb * TILE, TILE), TILE), cols].astype(F32)
             wide = wide * wide
             squares[:, cols] += wide[:8] + wide[8:]
         return carry
 
     lax.fori_loop(0, blocks, second_pass, 0)
-
-    packed = col[...]
-    missing = jnp.sum(jnp.bitwise_and(jnp.right_shift(packed, 24), 255), axis=0, keepdims=True)
-    het = jnp.sum(jnp.bitwise_and(jnp.right_shift(packed, 8), 255), axis=0, keepdims=True)
-    called = (rows - missing).astype(F32)
-    het = het.astype(F32)
-    share = jnp.sum(squares[...], axis=0, keepdims=True)
-    for p in range(nv):
-        cols = slice(p * slice_w, (p + 1) * slice_w)
-        samp_s[p, 0:1, :] = called[:, cols]
-        samp_s[p, 1:2, :] = het[:, cols]
-        samp_s[p, 2:3, :] = share[:, cols]
-        samp_s[p, 3:4, :] = jnp.zeros((1, slice_w), F32)
-    samp_r[b] = samp_s[b]
 
     def samp_copy(i, src, dst, target):
         return pltpu.make_async_remote_copy(
@@ -270,17 +281,34 @@
             device_id_type=MESH,
         )
 
-    for d in range(1, nv):
-        target = (b + d) % nv
-        samp_copy(0, samp_s.at[target], samp_r.at[b], target).start()
-
-    def y_copy(u, d):
-        target = (y + d) % ny
-        return pltpu.make_async_remote_copy(
-            src_ref=ysend.at[u, target],
-            dst_ref=yrecv.at[u, d - 1],
-            send_sem=ys_sem.at[u],
-            recv_sem=yr_sem.at[u],
+    def per_sample():
+        lax.fori_loop(0, blocks, square_pass, 0)
+        packed = col[...]
+        missing = jnp.sum(jnp.bitwise_and(jnp.right_shift(packed, 24), 255), axis=0, keepdims=True)
+        het = jnp.sum(jnp.bitwise_and(jnp.right_shift(packed, 8), 255), axis=0, keepdims=True)
+        called = (rows - missing).astype(F32)
+        het = het.astype(F32)
+        share = jnp.sum(squares[...], axis=0, keepdims=True)
+        for p in range(nv):
+            cols = slice(p * slice_w, (p + 1) * slice_w)
+            samp_s[p, 0:1, :] = called[:, cols]
+            samp_s[p, 1:2, :] = het[:, cols]
+            samp_s[p, 2:3, :] = share[:, cols]
+            samp_s[p, 3:4, :] = jnp.zeros((1, slice_w), F32)
+        samp_r[b] = samp_s[b]
+        for d in range(1, nv):
+            target = (b + d) % nv
+            samp_copy(0, samp_s.at[target], samp_r.at[b], target).start()
+
+    up, down, across = (y + 1) % ny, (y + ny - 1) % ny, (y + 2) % ny
+    lower, upper = pl.ds(0, nz // 2), pl.ds(nz // 2, nz // 2)
+
+    def y_copy(src, dst, sems, target):
+        return pltpu.make_async_remote_copy(
+            src_ref=src,
+            dst_ref=dst,
+            send_sem=sems[0],
+            recv_sem=sems[1],
             device_id=at(target, z),
             device_id_type=MESH,
         )
@@ -297,45 +325,63 @@
         )
 
     def y_start(u):
-        for d in range(1, ny):
-            y_copy(u, d).start()
-
-    def y_fold(u):
-        drain(yrecv.at[u], yr_sem.at[u])
-        part = ysend[u, y].astype(F32)
-        for d in range(ny - 1):
-            part = part + yrecv[u, d].astype(F32)
-        zsend[u] = part.astype(HALF)
+        sems = ya_s.at[u], ya_r.at[u]
+        y_copy(ysend.at[u, across, lower], yfar.at[u, 0], sems, up).start()
+        y_copy(ysend.at[u, across, upper], yfar.at[u, 1], sems, down).start()
+
+    def y_direct(u):
+        far, near = (ya_s.at[u], ya_r.at[u]), (yb_s.at[u], yb_r.at[u])
+        y_copy(ysend.at[u, up], ynear.at[u, 0], near, up).start()
+        y_copy(ysend.at[u, down], ynear.at[u, 1], near, down).start()
+        y_copy(ysend.at[u, across, lower], yfar.at[u, 0], far, across).start()
+        y_copy(ysend.at[u, across, upper], yfar.at[u, 1], far, across).start()
+
+    def y_relay(u):
+        drain(yfar.at[u], ya_r.at[u])
+        sems = yb_s.at[u], yb_r.at[u]
+        for slot, target, part in ((0, up, lower), (1, down, upper)):
+            both = decoded(ysend[u, target, part]) + decoded(yfar[u, slot])
+            ysend[u, target, part] = coded(both * (1.0 / STEPS**2))
+            y_copy(ysend.at[u, target], ynear.at[u, slot], sems, target).start()
+
+    def z_start(u, part):
+        zsend[u] = coded(part * (1.0 / STEPS**2))
         for d in range(1, nz):
             z_copy(u, d).start()
 
+    def y_fold_all(u):
+        drain(ynear.at[u], yb_r.at[u])
+        drain(yfar.at[u], ya_r.at[u])
+        part = decoded(ysend[u, y]) + decoded(ynear[u, 0]) + decoded(ynear[u, 1])
+        z_start(u, part + decoded(yfar[u]).reshape(nz, TILE, qw))
+
+    def y_fold(u):
+        drain(ynear.at[u], yb_r.at[u])
+        z_start(u, decoded(ysend[u, y]) + decoded(ynear[u, 0]) + decoded(ynear[u, 1]))
+
     def z_fold(u):
         drain(zrecv.at[u], zr_sem.at[u])
-        part = zsend[u, z].astype(F32)
+        part = decoded(zsend[u, z])
         for d in range(nz - 1):
-            part = part + zrecv[u, d].astype(F32)
-        fin[u] = part * (1.0 / GAIN)
+            part = part + decoded(zrecv[u, d])
+        fin[u] = part * (1.0 / STEPS**2)
 
     qw = rows // QUARTERS
 
     def group_rows(value, u):
-        value = (value * GAIN).astype(HALF).reshape(2, nz, 2, TILE, qw)
+        value = coded(value).reshape(2, nz, 2, TILE, qw)
         for yr in range(2):
             for hh in range(2):
                 ysend[u, 2 * yr + hh] = value[yr, :, hh]
 
     for pair in range(2):
-        acc[...] = jnp.zeros_like(acc)
-
-        def own(kc, carry):
-            left = scl[kc].reshape(rows, width)
-            right = scl[kc, pair * (blocks // 2) : (pair + 1) * (blocks // 2)]
-            acc[...] += lax.dot_general(
-                left, right.reshape(rows // 2, width), NT, preferred_element_type=F32
+        with jax.named_scope("own_dot"):
+            acc[...] = lax.dot_general(
+                scl[...],
+                scl[pair * (rows // 2) : (pair + 1) * (rows // 2)],
+                NT,
+                preferred_element_type=F32,
             )
-            return carry
-
-        lax.fori_loop(0, PARTS, own, 0)
         for j in range(2):
             group_rows(acc[:, j * qw : (j + 1) * qw], 2 * pair + j)
             y_start(2 * pair + j)
@@ -349,30 +395,34 @@
     def _():
         to_next.wait_recv()
         widen(2)
+
+    def y_begin(c, u):
+        @pl.when(c < QUARTERS - 1)
+        def _():
+            y_start(u)
+
+        @pl.when(c == QUARTERS - 1)
+        def _():
+            y_direct(u)
 
     def chunk_n(c):
         copy_n(c).wait_recv()
         for kc in range(half):
             roots = root_w[:, kc * width : (kc + 1) * width]
             for zz in range(nz):
-                recv_n[c, kc, zz] = scaled(
+                scl_n[zz * TILE : (zz + 1) * TILE, kc * width : (kc + 1) * width] = scaled(
                     recv_n[c, kc, zz],
                     roots,
                     bcast[1, 0, c // 2, zz, c % 2],
                     bcast[1, 1, c // 2, zz, c % 2],
                 )
-        out = jnp.zeros((nz * TILE, rows), F32)
-        for kc in range(half):
-            out = out + lax.dot_general(
-                recv_n[c, kc].reshape(nz * TILE, width),
-                scl[kc].reshape(rows, width),
-                NT,
-                preferred_element_type=F32,
-            )
-        out = (out * GAIN).astype(HALF)
+        out = lax.dot_general(
+            scl_n[...], scl[:, : half * width], NT, preferred_element_type=F32
+        )
+        out = coded(out)
         for q in range(QUARTERS):
             ysend[4 + c, q] = out[:, q * qw : (q + 1) * qw].reshape(nz, TILE, qw)
-        y_start(4 + c)
+        y_begin(c, 4 + c)
 
     def chunk_p(c):
         copy_p(c).wait_recv()
@@ -381,19 +431,15 @@
             for zz in range(nz // 2):
                 for hh in range(2):
                     spot = (c // 2, (c % 2) * (nz // 2) + zz, hh)
-                    recv_p[c, kc, zz, hh] = scaled(
+                    start = (2 * zz + hh) * TILE
+                    scl_p[start : start + TILE, kc * width : (kc + 1) * width] = scaled(
                         recv_p[c, kc, zz, hh], roots, bcast[(2, 0, *spot)], bcast[(2, 1, *spot)]
                     )
-        out = jnp.zeros((rows, qw), F32)
-        for kc in range(half):
-            out = out + lax.dot_general(
-                scl[half + kc].reshape(rows, width),
-                recv_p[c, kc].reshape(qw, width),
-                NT,
-                preferred_element_type=F32,
-            )
+        out = lax.dot_general(
+            scl[:, half * width :], scl_p[...], NT, preferred_element_type=F32
+        )
         group_rows(out, 8 + c)
-        y_start(8 + c)
+        y_begin(c, 8 + c)
 
     def n_copy(c):
         return pltpu.make_async_remote_copy(
@@ -447,25 +493,44 @@
             def _():
                 chunk_p(c)
 
-        @pl.when(c == 0)
-        def _():
-            for u in range(QUARTERS):
-                y_fold(u)
-
-        @pl.when((c >= 1) & (c <= QUARTERS))
-        def _():
+        def both(at_c, action):
             @pl.when(b < nv - 1)
             def _():
-                y_fold(4 + c - 1)
+                action(QUARTERS + at_c)
 
             @pl.when(b > 0)
             def _():
-                y_fold(8 + c - 1)
+                action(2 * QUARTERS + at_c)
+
+        def own_units(action):
+            for u in range(QUARTERS):
+                action(u)
+
+        @pl.when(c == 0)
+        def _():
+            own_units(y_relay)
 
         @pl.when(c == 1)
         def _():
-            for u in range(QUARTERS):
-                z_fold(u)
+            both(0, y_relay)
+
+        @pl.when(c == 2)
+        def _():
+            own_units(y_fold)
+            both(1, y_relay)
+
+        @pl.when(c == 3)
+        def _():
+            per_sample()
+            both(2, y_relay)
+            both(0, y_fold)
+            both(1, y_fold)
+
+        @pl.when(c == 4)
+        def _():
+            both(3, y_fold_all)
+            both(2, y_fold)
+            own_units(z_fold)
 
             @pl.when(y == 0)
             def _():
@@ -475,37 +540,33 @@
             def _():
                 o_copy().start()
 
+        @pl.when(c == 6)
+        def _():
             drain(samp_r.at[pl.ds(0, nv - 1)], samp_rs.at[0])
             samp_g[b] = sum(samp_r[p] for p in range(nv))
             for d in range(1, nv):
                 samp_copy(1, samp_g.at[b], samp_g.at[b], (b + d) % nv).start()
 
-        @pl.when(c >= 2)
-        def _():
+        @pl.when(c > QUARTERS)
+        def _():
+            both(c - QUARTERS - 1, z_fold)
+
             @pl.when(b < nv - 1)
             def _():
-                z_fold(4 + c - 2)
-                n_final(c - 2)
-
-            @pl.when(b > 0)
-            def _():
-                z_fold(8 + c - 2)
+                n_final(c - QUARTERS - 1)
 
         return carry
 
-    lax.fori_loop(0, QUARTERS + 2, step, 0)
+    lax.fori_loop(0, 2 * QUARTERS + 1, step, 0)
 
     @pl.when(b > 0)
     def _():
         p_copy().start()
 
     drain(cnt_y.at[pl.ds(0, ny - 1)], stat_r.at[3])
-    count_o[...] = sum(cnt_y[i] for i in range(ny)).astype(jnp.int32)
+    stat_o[4:8, :] = sum(cnt_y[i] for i in range(ny))
     drain(samp_g.at[pl.ds(0, nv - 1)], samp_rs.at[1])
-    for p in range(nv):
-        cols = slice(p * slice_w, (p + 1) * slice_w)
-        calls_o[:, cols] = samp_g[p, 0:2, :].astype(jnp.int32)
-        share_o[:, cols] = samp_g[p, 2:3, :] * (samples_all / (nv * rows))
+    samp_o[...] = samp_g[...]
 
     @pl.when(y == 0)
     def _():
@@ -547,7 +608,8 @@
     drain(samp_g.at[pl.ds(0, nv - 1)], samp_ss.at[1])
 
     def sent(u, carry):
-        drain(yrecv.at[u], ys_sem.at[u])
+        drain(yfar.at[u], ya_s.at[u])
+        drain(ynear.at[u], yb_s.at[u])
         drain(zrecv.at[u], zs_sem.at[u])
         return carry
 
@@ -575,6 +637,18 @@
         p_copy().wait_send()
         for c in range(QUARTERS):
             copy_n(c).wait_send()
+
+
+def deliver(ratio, stat_ref, ld_ref, samp_ref, mean_o, var_o, count_o, ld_o, calls_o, share_o):
+    mean_o[...] = stat_ref[0:1, :]
+    var_o[...] = stat_ref[1:2, :]
+    count_o[...] = stat_ref[4:8, :].astype(jnp.int32)
+    ld_o[...] = ld_ref[...]
+    slice_w = samp_ref.shape[2]
+    for p in range(samp_ref.shape[0]):
+        cols = slice(p * slice_w, (p + 1) * slice_w)
+        calls_o[:, cols] = samp_ref[p, 0:2, :].astype(jnp.int32)
+        share_o[:, cols] = samp_ref[p, 2:3, :] * ratio
 
 
 def on_device(ny, nz, nv, genotypes, weights):
@@ -586,23 +660,18 @@
     vmem = pl.BlockSpec(memory_space=pltpu.VMEM)
     dma = pltpu.SemaphoreType.DMA
     units = 3 * QUARTERS
-    shapes = (
-        ((1, rows), F32),
-        ((1, rows), F32),
-        ((4, rows), jnp.int32),
-        ((2 * TILE, rows), F32),
-        ((2, cols), jnp.int32),
-        ((1, cols), F32),
-    )
-    mean, var, counts, ld, calls, share = pl.pallas_call(
-        functools.partial(kernel, ny, nz, nv, cols * ny * nz),
+    shapes = (((8, rows), F32), ((2 * TILE, rows), F32), ((nv, 4, slice_w), F32))
+    held = pl.pallas_call(
+        functools.partial(kernel, ny, nz, nv),
         out_shape=[jax.ShapeDtypeStruct(s, t) for s, t in shapes],
         in_specs=[pl.BlockSpec(memory_space=pl.ANY), vmem],
         out_specs=[vmem] * len(shapes),
         scratch_shapes=[
             pltpu.VMEM((blocks, TILE, cols), jnp.int32),
             pltpu.VMEM((PARTS, 2, nz, 2, TILE, width), bf16),
-            pltpu.VMEM((PARTS, blocks, TILE, width), bf16),
+            pltpu.VMEM((rows, cols), bf16),
+            pltpu.VMEM((nz * TILE, half * width), bf16),
+            pltpu.VMEM((qw, half * width), bf16),
             pltpu.VMEM((QUARTERS, half, nz, TILE, width), bf16),
             pltpu.VMEM((QUARTERS, half, nz // 2, 2, TILE, width), bf16),
             pltpu.VMEM((TILE, cols), F32),
@@ -622,7 +691,8 @@
             pltpu.VMEM((nv, 4, slice_w), F32),
             pltpu.VMEM((rows, rows // 2), F32),
             pltpu.VMEM((units, ny, nz, TILE, qw), HALF),
-            pltpu.VMEM((units, ny - 1, nz, TILE, qw), HALF),
+            pltpu.VMEM((units, 2, nz // 2, TILE, qw), HALF),
+            pltpu.VMEM((units, 2, nz, TILE, qw), HALF),
             pltpu.VMEM((units, nz, TILE, qw), HALF),
             pltpu.VMEM((units, nz - 1, TILE, qw), HALF),
             pltpu.VMEM((units, TILE, qw), F32),
@@ -644,6 +714,8 @@
             dma((units,)),
             dma((units,)),
             dma((units,)),
+            dma((units,)),
+            dma((units,)),
             dma((1,)),
             dma((2,)),
             dma((QUARTERS,)),
@@ -655,6 +727,20 @@
             collective_id=0, has_side_effects=True, vmem_limit_bytes=60 * 2**20
         ),
     )(genotypes.reshape(blocks, TILE, cols), weights.reshape(1, cols))
+    shapes = (
+        ((1, rows), F32),
+        ((1, rows), F32),
+        ((4, rows), jnp.int32),
+        ((2 * TILE, rows), F32),
+        ((2, cols), jnp.int32),
+        ((1, cols), F32),
+    )
+    mean, var, counts, ld, calls, share = pl.pallas_call(
+        functools.partial(deliver, ny * nz * cols / (nv * rows)),
+        out_shape=[jax.ShapeDtypeStruct(s, t) for s, t in shapes],
+        in_specs=[vmem] * 3,
+        out_specs=[vmem] * len(shapes),
+    )(*held)
     return (
         mean.reshape(rows),
         var.reshape(rows),

time: 80.8 us -> 57.7 us (0.71)
  Pallas kernels: 71.6 us -> 56.9 us
  local copies, waits for them, and re-layouts: 7.96 us -> 0 us
    pallas_call x1 -> x2, Pallas kernels: 71.6 us -> 56.9 us  [the longest x1 55.3 us: on_device(): pl.pallas_call(functools.partial(kernel, ny, nz, nv), out_shape=[jax.Shap...]
    unnamed x6 -> x0, local copies, waits for them, and re-layouts: 7.96 us -> none
where the time goes in v2:
time: 57.7 us; the launch traced here: 57.5 us
  Pallas kernels  56.9 us (99%)
  between operations  0.64 us (1%)
    pallas_call x1, Pallas kernels, on_device(): pl.pallas_call(functools.partial(kernel, ny, nz, nv), out_shape=[jax.Shap...  55.3 us
    pallas_call x1, Pallas kernels, on_device(): pl.pallas_call(functools.partial(deliver, ny * nz * cols / (nv * rows)),...  1.56 us

profile of v2, /device:TPU:19, one launch (start us, length us, event | category | flops | bytes accessed | tf_op | source)
XLA Modules:
  0.0 57.5 jit_solution(8127719397422469097)
XLA Ops:
  0.6 55.3 %shard_map.73 = (f32[8,512]{1,0:T(8,128)}, f32[32,512]{1,0:T(8,128)}, f32[8,4,512]{2,1,0:T(4,128)}) custom-call(s32[32,16,4096]{2,1,0:T(8,128)} %bitcast.5, f32[1,4096]{1,0:T(1,128)} %bitcast.6), custom_call_target="tpu_custom_call" | custom-call | tf_op jit(solution)/shard_map/pallas_call | solution.py:664
  56.0 1.6 %shard_map.74 = (f32[1,512]{1,0:T(1,128)}, f32[1,512]{1,0:T(1,128)}, s32[4,512]{1,0:T(4,128)}, f32[32,512]{1,0:T(8,128)}, s32[2,4096]{1,0:T(2,128)}, /*index=5*/f32[1,4096]{1,0:T(1,128)}) custom-call(f32[8,512]{1,0:T(8,128)} %get-tuple-element.15.stat_ref, f32[32,512]{1,0:T(8,128)} %get-tuple-element.16.ld_ref, f32[8,4,512]{2,1,0:T(4,128)} %get-tuple-element.17.samp_ref), custom_call_target="tpu_custom_call" | custom-call | tf_op jit(solution)/shard_map/pallas_call | solution.py:738

commit v3 on v2

--- a/solution.py
+++ b/solution.py
@@ -16,6 +16,7 @@
 STEPS = 32000.0
 F32 = jnp.float32
 NT = (((1,), (1,)), ((), ()))
+NN = (((1,), (0,)), ((), ()))
 
 
 def drain(ref, sem):
@@ -44,10 +45,10 @@
     ny, nz, nv,
     g_hbm, w_ref,
     stat_o, ld_o, samp_o,
-    gbuf, raw, scl, scl_n, scl_p, recv_n, recv_p, wide_w, root_w, moments, codes, col, squares,
+    gbuf, raw, scl, scl_t, scl_n, scl_p, acc_n, acc_m, recv_q, recv_n, recv_p, wide_w, root_w, moments, codes, col, squares,
     crit_z, crit_y, cnt_z, cnt_y, mf, bcast, samp_s, samp_r, samp_g, acc,
     ysend, yfar, ynear, zsend, zrecv, fin, fin_o, fin_n, fin_p,
-    gsem, xs_n, xs_p, xr_n, xr_p, stat_s, stat_r, mf_s, mf_r, samp_ss, samp_rs,
+    gsem, xs_q, xr_q, xs_n, xs_p, xr_n, xr_p, stat_s, stat_r, mf_s, mf_r, samp_ss, samp_rs,
     ya_s, ya_r, yb_s, yb_r, zs_sem, zr_sem, fo_s, fo_r, fn_s, fn_r, fp_s, fp_r,
 ):
     k, b = lax.axis_index("samples"), lax.axis_index("variants")
@@ -128,9 +129,16 @@
         codes[rb] = sum_c
         return carry
 
+    odd = b % 2
+
     def copy_n(c):
         return pltpu.make_async_remote_copy(
-            src_ref=raw.at[pl.ds(0, half), c // 2, :, c % 2],
+            src_ref=raw.at[
+                pl.ds(odd * (c % 2) * half, half),
+                (1 - odd) * (c // 2),
+                :,
+                odd * (c // 2) + (1 - odd) * (c % 2),
+            ],
             dst_ref=recv_n.at[c],
             send_sem=xs_n.at[c],
             recv_sem=xr_n.at[c],
@@ -138,15 +146,21 @@
             device_id_type=MESH,
         )
 
+    def copy_rows(c, base, dst, send_sems, recv_sems):
+        return pltpu.make_async_remote_copy(
+            src_ref=raw.at[pl.ds(base, half), c // 2, pl.ds((c % 2) * (nz // 2), nz // 2)],
+            dst_ref=dst.at[c],
+            send_sem=send_sems.at[c],
+            recv_sem=recv_sems.at[c],
+            device_id={"variants": jnp.minimum(b + 1, nv - 1)},
+            device_id_type=MESH,
+        )
+
     def copy_p(c):
-        return pltpu.make_async_remote_copy(
-            src_ref=raw.at[pl.ds(half, half), c // 2, pl.ds((c % 2) * (nz // 2), nz // 2)],
-            dst_ref=recv_p.at[c],
-            send_sem=xs_p.at[c],
-            recv_sem=xr_p.at[c],
-            device_id={"variants": jnp.minimum(b + 1, nv - 1)},
-            device_id_type=MESH,
-        )
+        return copy_rows(c, half, recv_p, xs_p, xr_p)
+
+    def copy_q(c):
+        return copy_rows(c, 0, recv_q, xs_q, xr_q)
 
     def wait_part(part):
         group = pl.ds(part * (blocks // 8), blocks // 8)
@@ -161,6 +175,10 @@
         @pl.when(b < nv - 1)
         def _():
             copy_p(c).start()
+
+        @pl.when(odd == 0)
+        def _():
+            copy_q(c).start()
 
         @pl.when(b > 0)
         def _():
@@ -199,7 +217,6 @@
     crit_y[y] = sum(crit_z[i] for i in range(nz))
     for d in range(1, ny):
         push(crit_y.at[y], crit_y.at[y], 2, at((y + d) % ny, z)).start()
-    start_chunk(2)
     drain(crit_y.at[pl.ds(0, ny - 1)], stat_r.at[2])
     total = sum(crit_y[i] for i in range(ny))
     w_sum, first_total, second_total = total[0:1], total[1:2], total[2:3]
@@ -233,6 +250,7 @@
     def _():
         to_next.start()
 
+    start_chunk(2)
     start_chunk(3)
 
     def widen(slot):
@@ -376,18 +394,28 @@
 
     for pair in range(2):
         with jax.named_scope("own_dot"):
-            acc[...] = lax.dot_general(
-                scl[...],
-                scl[pair * (rows // 2) : (pair + 1) * (rows // 2)],
-                NT,
-                preferred_element_type=F32,
-            )
+            if pair == 0:
+                acc[...] = lax.dot_general(
+                    scl[...], scl[: rows // 2], NT, preferred_element_type=F32
+                )
+            else:
+                acc[: rows // 2] = acc[rows // 2 :].T
+                acc[rows // 2 :] = lax.dot_general(
+                    scl[rows // 2 :], scl[rows // 2 :], NT, preferred_element_type=F32
+                )
         for j in range(2):
             group_rows(acc[:, j * qw : (j + 1) * qw], 2 * pair + j)
             y_start(2 * pair + j)
 
     @pl.when(b < nv - 1)
     def _():
+        with jax.named_scope("turn"):
+            scl_t[: half * width] = scl[:, : half * width].T
+
+            @pl.when(odd == 0)
+            def _():
+                scl_t[half * width :] = scl[:, half * width :].T
+
         to_prev.wait_recv()
         widen(1)
 
@@ -397,49 +425,96 @@
         widen(2)
 
     def y_begin(c, u):
-        @pl.when(c < QUARTERS - 1)
+        @pl.when(c < QUARTERS - 2)
         def _():
             y_start(u)
 
-        @pl.when(c == QUARTERS - 1)
+        @pl.when(c >= QUARTERS - 2)
         def _():
             y_direct(u)
 
     def chunk_n(c):
         copy_n(c).wait_recv()
+        side = (1 - odd) * (c % 2)
+        yr, hh = odd * (c // 2), odd * (c % 2) + (1 - odd) * (c // 2)
+        base = pl.multiple_of(side * half * width, half * width)
         for kc in range(half):
-            roots = root_w[:, kc * width : (kc + 1) * width]
+            roots = root_w[:, pl.ds(pl.multiple_of(base + kc * width, width), width)]
             for zz in range(nz):
                 scl_n[zz * TILE : (zz + 1) * TILE, kc * width : (kc + 1) * width] = scaled(
-                    recv_n[c, kc, zz],
-                    roots,
-                    bcast[1, 0, c // 2, zz, c % 2],
-                    bcast[1, 1, c // 2, zz, c % 2],
+                    recv_n[c, kc, zz], roots, bcast[1, 0, yr, zz, hh], bcast[1, 1, yr, zz, hh]
                 )
-        out = lax.dot_general(
-            scl_n[...], scl[:, : half * width], NT, preferred_element_type=F32
-        )
+        acc_n[...] = lax.dot_general(
+            scl_n[...], scl_t[pl.ds(base, half * width)], NN, preferred_element_type=F32
+        )
+
+    def pack_n(c, u, out):
         out = coded(out)
         for q in range(QUARTERS):
-            ysend[4 + c, q] = out[:, q * qw : (q + 1) * qw].reshape(nz, TILE, qw)
-        y_begin(c, 4 + c)
-
-    def chunk_p(c):
-        copy_p(c).wait_recv()
+            ysend[u, q] = out[:, q * qw : (q + 1) * qw].reshape(nz, TILE, qw)
+        y_begin(c, u)
+
+    def turn_p(c, buf, base):
         for kc in range(half):
-            roots = root_w[:, (half + kc) * width : (half + kc + 1) * width]
+            cols = slice((base + kc) * width, (base + kc + 1) * width)
+            roots = root_w[:, cols]
             for zz in range(nz // 2):
                 for hh in range(2):
                     spot = (c // 2, (c % 2) * (nz // 2) + zz, hh)
                     start = (2 * zz + hh) * TILE
-                    scl_p[start : start + TILE, kc * width : (kc + 1) * width] = scaled(
-                        recv_p[c, kc, zz, hh], roots, bcast[(2, 0, *spot)], bcast[(2, 1, *spot)]
+                    scl_p[start : start + TILE, cols] = scaled(
+                        buf[c, kc, zz, hh], roots, bcast[(2, 0, *spot)], bcast[(2, 1, *spot)]
                     )
+
+    def chunk_p(c):
+        copy_p(c).wait_recv()
+        turn_p(c, recv_p, half)
         out = lax.dot_general(
-            scl[:, half * width :], scl_p[...], NT, preferred_element_type=F32
+            scl[:, half * width :], scl_p[:, half * width :], NT, preferred_element_type=F32
         )
         group_rows(out, 8 + c)
         y_begin(c, 8 + c)
+
+    def chunk_q(c):
+        copy_p(c).wait_recv()
+        turn_p(c, recv_p, half)
+        copy_q(c).wait_recv()
+        turn_p(c, recv_q, 0)
+        out = lax.dot_general(
+            scl[rows // 2 :], scl_p[...], NT, preferred_element_type=F32
+        )
+        out = coded(out).reshape(nz, 2, TILE, qw)
+        for hh in range(2):
+            ysend[8 + c // 2, 2 * hh + c % 2] = out[:, hh]
+
+        @pl.when(c % 2 == 1)
+        def _():
+            y_begin(c, 8 + c // 2)
+
+    def chunk(c):
+        @pl.when(b < nv - 1)
+        def _():
+            chunk_n(c)
+
+            @pl.when(odd == 1)
+            def _():
+                pack_n(c, 4 + c, acc_n[...])
+
+            @pl.when((odd == 0) & (c % 2 == 1))
+            def _():
+                pack_n(c, 4 + c // 2, acc_m[...] + acc_n[...])
+
+            @pl.when((odd == 0) & (c % 2 == 0))
+            def _():
+                acc_m[...] = acc_n[...]
+
+        @pl.when((odd == 0) & (b > 0))
+        def _():
+            chunk_p(c)
+
+        @pl.when(odd == 1)
+        def _():
+            chunk_q(c)
 
     def n_copy(c):
         return pltpu.make_async_remote_copy(
@@ -471,6 +546,16 @@
             device_id_type=MESH,
         )
 
+    def q_copy(k):
+        return pltpu.make_async_remote_copy(
+            src_ref=fin.at[8 + k],
+            dst_ref=fin_p.at[y // 2, 2 * k + y % 2],
+            send_sem=fp_s.at[k],
+            recv_sem=fp_r.at[y // 2],
+            device_id={"samples": 3 * nz + z, "variants": jnp.maximum(b - 1, 0)},
+            device_id_type=MESH,
+        )
+
     def n_final(c):
         owner = 2 + c // 2
 
@@ -485,22 +570,20 @@
     def step(c, carry):
         @pl.when(c < QUARTERS)
         def _():
-            @pl.when(b < nv - 1)
-            def _():
-                chunk_n(c)
-
-            @pl.when(b > 0)
-            def _():
-                chunk_p(c)
-
-        def both(at_c, action):
-            @pl.when(b < nv - 1)
-            def _():
-                action(QUARTERS + at_c)
-
-            @pl.when(b > 0)
-            def _():
-                action(2 * QUARTERS + at_c)
+            chunk(c)
+
+        def both(i, action):
+            @pl.when((odd == 1) & (b < nv - 1))
+            def _():
+                action(QUARTERS + i)
+
+            @pl.when((odd == 0) & (b > 0))
+            def _():
+                action(2 * QUARTERS + i)
+
+            @pl.when(i % 2 == 1)
+            def _():
+                action((1 + odd) * QUARTERS + i // 2)
 
         def own_units(action):
             for u in range(QUARTERS):
@@ -512,6 +595,7 @@
 
         @pl.when(c == 1)
         def _():
+            per_sample()
             both(0, y_relay)
 
         @pl.when(c == 2)
@@ -521,15 +605,13 @@
 
         @pl.when(c == 3)
         def _():
-            per_sample()
-            both(2, y_relay)
             both(0, y_fold)
             both(1, y_fold)
 
         @pl.when(c == 4)
         def _():
+            both(2, y_fold_all)
             both(3, y_fold_all)
-            both(2, y_fold)
             own_units(z_fold)
 
             @pl.when(y == 0)
@@ -540,7 +622,7 @@
             def _():
                 o_copy().start()
 
-        @pl.when(c == 6)
+        @pl.when(c == 4)
         def _():
             drain(samp_r.at[pl.ds(0, nv - 1)], samp_rs.at[0])
             samp_g[b] = sum(samp_r[p] for p in range(nv))
@@ -549,19 +631,29 @@
 
         @pl.when(c > QUARTERS)
         def _():
-            both(c - QUARTERS - 1, z_fold)
-
-            @pl.when(b < nv - 1)
-            def _():
-                n_final(c - QUARTERS - 1)
+            i = c - QUARTERS - 1
+            both(i, z_fold)
+
+            @pl.when((odd == 1) & (b < nv - 1))
+            def _():
+                n_final(i)
+
+            @pl.when((odd == 0) & (i % 2 == 1))
+            def _():
+                n_final(i // 2)
 
         return carry
 
     lax.fori_loop(0, 2 * QUARTERS + 1, step, 0)
 
-    @pl.when(b > 0)
+    @pl.when((odd == 0) & (b > 0))
     def _():
         p_copy().start()
+
+    @pl.when(odd == 1)
+    def _():
+        for k_unit in range(2):
+            q_copy(k_unit).start()
 
     drain(cnt_y.at[pl.ds(0, ny - 1)], stat_r.at[3])
     stat_o[4:8, :] = sum(cnt_y[i] for i in range(ny))
@@ -583,22 +675,38 @@
             for q in range(QUARTERS):
                 ld_o[h * TILE : (h + 1) * TILE, q * qw : (q + 1) * qw] = fin_o[h, q]
 
-    @pl.when(y >= 2)
-    def _():
-        @pl.when(b < nv - 1)
-        def _():
-            for h in range(2):
-                drain(fin_n.at[h, pl.ds(0, ny - 1)], fn_r.at[h])
-                drain(fin_p.at[h], fp_r.at[h])
-            for h in range(2):
-                for q in range(QUARTERS):
-                    ld_o[h * TILE : (h + 1) * TILE, q * qw : (q + 1) * qw] = (
-                        fin_n[h, q] + fin_p[h, q]
-                    )
-
-        @pl.when(b == nv - 1)
-        def _():
-            ld_o[...] = jnp.zeros_like(ld_o)
+    def wait_n():
+        for h in range(2):
+            drain(fin_n.at[h, pl.ds(0, ny - 1)], fn_r.at[h])
+
+    def wait_p():
+        for h in range(2):
+            drain(fin_p.at[h], fp_r.at[h])
+
+    def write(value):
+        for h in range(2):
+            for q in range(QUARTERS):
+                ld_o[h * TILE : (h + 1) * TILE, q * qw : (q + 1) * qw] = value(h, q)
+
+    @pl.when((y >= 2) & (odd == 1) & (b < nv - 1))
+    def _():
+        wait_n()
+        wait_p()
+        write(lambda h, q: fin_n[h, q] + fin_p[h, q])
+
+    @pl.when((y == 2) & (odd == 0))
+    def _():
+        wait_n()
+        write(lambda h, q: fin_n[h, q])
+
+    @pl.when((y == 3) & (odd == 0))
+    def _():
+        wait_p()
+        write(lambda h, q: fin_p[h, q])
+
+    @pl.when((y >= 2) & (b == nv - 1))
+    def _():
+        ld_o[...] = jnp.zeros_like(ld_o)
 
     drain(crit_z.at[pl.ds(0, nz - 1)], stat_s.at[0])
     drain(cnt_z.at[pl.ds(0, nz - 1)], stat_s.at[1])
@@ -619,24 +727,46 @@
     def _():
         o_copy().wait_send()
 
+    def sent_n(count):
+        lax.fori_loop(QUARTERS, QUARTERS + count, sent, 0)
+        for c in range(count):
+
+            @pl.when(y != 2 + c // 2)
+            def _():
+                n_copy(c).wait_send()
+
+    @pl.when((odd == 1) & (b < nv - 1))
+    def _():
+        sent_n(QUARTERS)
+
+    @pl.when(odd == 0)
+    def _():
+        sent_n(2)
+        for c in range(QUARTERS):
+            copy_q(c).wait_send()
+
     @pl.when(b < nv - 1)
     def _():
-        lax.fori_loop(QUARTERS, 2 * QUARTERS, sent, 0)
         to_next.wait_send()
         for c in range(QUARTERS):
             copy_p(c).wait_send()
 
-            @pl.when(y != 2 + c // 2)
-            def _():
-                n_copy(c).wait_send()
-
     @pl.when(b > 0)
     def _():
-        lax.fori_loop(2 * QUARTERS, 3 * QUARTERS, sent, 0)
         to_prev.wait_send()
-        p_copy().wait_send()
         for c in range(QUARTERS):
             copy_n(c).wait_send()
+
+    @pl.when((odd == 0) & (b > 0))
+    def _():
+        lax.fori_loop(2 * QUARTERS, 3 * QUARTERS, sent, 0)
+        p_copy().wait_send()
+
+    @pl.when(odd == 1)
+    def _():
+        lax.fori_loop(2 * QUARTERS, 2 * QUARTERS + 2, sent, 0)
+        for k_unit in range(2):
+            q_copy(k_unit).wait_send()
 
 
 def deliver(ratio, stat_ref, ld_ref, samp_ref, mean_o, var_o, count_o, ld_o, calls_o, share_o):
@@ -670,8 +800,12 @@
             pltpu.VMEM((blocks, TILE, cols), jnp.int32),
             pltpu.VMEM((PARTS, 2, nz, 2, TILE, width), bf16),
             pltpu.VMEM((rows, cols), bf16),
+            pltpu.VMEM((cols, rows), bf16),
             pltpu.VMEM((nz * TILE, half * width), bf16),
-            pltpu.VMEM((qw, half * width), bf16),
+            pltpu.VMEM((qw, cols), bf16),
+            pltpu.VMEM((nz * TILE, rows), F32),
+            pltpu.VMEM((nz * TILE, rows), F32),
+            pltpu.VMEM((QUARTERS, half, nz // 2, 2, TILE, width), bf16),
             pltpu.VMEM((QUARTERS, half, nz, TILE, width), bf16),
             pltpu.VMEM((QUARTERS, half, nz // 2, 2, TILE, width), bf16),
             pltpu.VMEM((TILE, cols), F32),
@@ -704,6 +838,8 @@
             dma((QUARTERS,)),
             dma((QUARTERS,)),
             dma((QUARTERS,)),
+            dma((QUARTERS,)),
+            dma((QUARTERS,)),
             dma((4,)),
             dma((4,)),
             dma((2,)),
@@ -720,7 +856,7 @@
             dma((2,)),
             dma((QUARTERS,)),
             dma((2,)),
-            dma((1,)),
+            dma((2,)),
             dma((2,)),
         ],
         compiler_params=pltpu.CompilerParams(

time: 57.7 us -> 52.5 us (0.910)
  Pallas kernels: 56.9 us -> 51.7 us
    pallas_call x1, Pallas kernels: 55.3 us -> 50.1 us  [on_device(): pl.pallas_call(functools.partial(kernel, ny, nz, nv), out_shape=[jax.Shap...]
where the time goes in v3:
time: 52.5 us; the launch traced here: 52.3 us
  Pallas kernels  51.7 us (98%)
  between operations  0.64 us (1%)
    pallas_call x1, Pallas kernels, on_device(): pl.pallas_call(functools.partial(kernel, ny, nz, nv), out_shape=[jax.Shap...  50.1 us
    pallas_call x1, Pallas kernels, on_device(): pl.pallas_call(functools.partial(deliver, ny * nz * cols / (nv * rows)),...  1.56 us

profile of v3, /device:TPU:19, one launch (start us, length us, event | category | flops | bytes accessed | tf_op | source)
XLA Modules:
  0.0 52.3 jit_solution(6308558096770457631)
XLA Ops:
  0.6 50.1 %shard_map.73 = (f32[8,512]{1,0:T(8,128)}, f32[32,512]{1,0:T(8,128)}, f32[8,4,512]{2,1,0:T(4,128)}) custom-call(s32[32,16,4096]{2,1,0:T(8,128)} %bitcast.5, f32[1,4096]{1,0:T(1,128)} %bitcast.6), custom_call_target="tpu_custom_call" | custom-call | tf_op jit(solution)/shard_map/pallas_call | solution.py:794
  50.7 1.6 %shard_map.74 = (f32[1,512]{1,0:T(1,128)}, f32[1,512]{1,0:T(1,128)}, s32[4,512]{1,0:T(4,128)}, f32[32,512]{1,0:T(8,128)}, s32[2,4096]{1,0:T(2,128)}, /*index=5*/f32[1,4096]{1,0:T(1,128)}) custom-call(f32[8,512]{1,0:T(8,128)} %get-tuple-element.15.stat_ref, f32[32,512]{1,0:T(8,128)} %get-tuple-element.16.ld_ref, f32[8,4,512]{2,1,0:T(4,128)} %get-tuple-element.17.samp_ref), custom_call_target="tpu_custom_call" | custom-call | tf_op jit(solution)/shard_map/pallas_call | solution.py:874

commit v4 on v3

--- a/solution.py
+++ b/solution.py
@@ -21,6 +21,10 @@
 
 def drain(ref, sem):
     pltpu.make_async_copy(ref, ref, sem).wait()
+
+
+def far_first(size):
+    return sorted(range(1, size), key=lambda d: -min(d, size - d))
 
 
 def folded(value):
@@ -72,21 +76,21 @@
     def greet(device):
         pl.semaphore_signal(barrier, inc=1, device_id=device, device_id_type=MESH)
 
-    for d in range(1, ny):
+    for d in far_first(nz):
+        greet(at(y, (z + d) % nz))
+    for d in far_first(ny):
         greet(at((y + d) % ny, z))
-    for d in range(1, nz):
-        greet(at(y, (z + d) % nz))
     for d in range(1, nv):
         greet({"variants": (b + d) % nv})
 
     @pl.when(b > 0)
     def _():
-        for d in range(1, ny):
+        for d in far_first(ny):
             greet({"samples": ((y + d) % ny) * nz + z, "variants": b - 1})
 
     @pl.when(b < nv - 1)
     def _():
-        for d in range(1, ny):
+        for d in far_first(ny):
             greet({"samples": ((y + d) % ny) * nz + z, "variants": b + 1})
 
     wide_w[...] = jnp.broadcast_to(w_ref[...], wide_w.shape)
@@ -201,7 +205,7 @@
         crit_z[z, q : q + 1, :] = to_row(moments[q])
     crit_z[z, 3:4, :] = jnp.zeros((1, rows), F32)
     pl.semaphore_wait(barrier, (ny - 1) + (nz - 1) + (nv - 1) + neighbours)
-    for d in range(1, nz):
+    for d in far_first(nz):
         push(crit_z.at[z], crit_z.at[z], 0, at(y, (z + d) % nz)).start()
     start_chunk(0)
     start_chunk(1)
@@ -210,12 +214,12 @@
     for level in range(4):
         field = jnp.bitwise_and(jnp.right_shift(fields, 8 * level), 255)
         cnt_z[z, level : level + 1, :] = to_row(field.astype(F32))
-    for d in range(1, nz):
+    for d in far_first(nz):
         push(cnt_z.at[z], cnt_z.at[z], 1, at(y, (z + d) % nz)).start()
 
     drain(crit_z.at[pl.ds(0, nz - 1)], stat_r.at[0])
     crit_y[y] = sum(crit_z[i] for i in range(nz))
-    for d in range(1, ny):
+    for d in far_first(ny):
         push(crit_y.at[y], crit_y.at[y], 2, at((y + d) % ny, z)).start()
     drain(crit_y.at[pl.ds(0, ny - 1)], stat_r.at[2])
     total = sum(crit_y[i] for i in range(ny))
@@ -267,7 +271,7 @@
 
     drain(cnt_z.at[pl.ds(0, nz - 1)], stat_r.at[1])
     cnt_y[y] = sum(cnt_z[i] for i in range(nz))
-    for d in range(1, ny):
+    for d in far_first(ny):
         push(cnt_y.at[y], cnt_y.at[y], 3, at((y + d) % ny, z)).start()
 
     def second_pass(rb, carry):
@@ -349,10 +353,10 @@
 
     def y_direct(u):
         far, near = (ya_s.at[u], ya_r.at[u]), (yb_s.at[u], yb_r.at[u])
+        y_copy(ysend.at[u, across, lower], yfar.at[u, 0], far, across).start()
+        y_copy(ysend.at[u, across, upper], yfar.at[u, 1], far, across).start()
         y_copy(ysend.at[u, up], ynear.at[u, 0], near, up).start()
         y_copy(ysend.at[u, down], ynear.at[u, 1], near, down).start()
-        y_copy(ysend.at[u, across, lower], yfar.at[u, 0], far, across).start()
-        y_copy(ysend.at[u, across, upper], yfar.at[u, 1], far, across).start()
 
     def y_relay(u):
         drain(yfar.at[u], ya_r.at[u])
@@ -364,7 +368,7 @@
 
     def z_start(u, part):
         zsend[u] = coded(part * (1.0 / STEPS**2))
-        for d in range(1, nz):
+        for d in far_first(nz):
             z_copy(u, d).start()
 
     def y_fold_all(u):

time: 52.5 us -> 52.2 us (level)
  no operation moved by 1% of the time
where the time goes in v4:
time: 52.2 us; the launch traced here: 52 us
  Pallas kernels  51.4 us (98%)
  between operations  0.64 us (1%)
    pallas_call x1, Pallas kernels, on_device(): pl.pallas_call(functools.partial(kernel, ny, nz, nv), out_shape=[jax.Shap...  49.8 us
    pallas_call x1, Pallas kernels, on_device(): pl.pallas_call(functools.partial(deliver, ny * nz * cols / (nv * rows)),...  1.56 us

profile of v4, /device:TPU:19, one launch (start us, length us, event | category | flops | bytes accessed | tf_op | source)
XLA Modules:
  0.0 52.0 jit_solution(10374642450745775800)
XLA Ops:
  0.6 49.8 %shard_map.73 = (f32[8,512]{1,0:T(8,128)}, f32[32,512]{1,0:T(8,128)}, f32[8,4,512]{2,1,0:T(4,128)}) custom-call(s32[32,16,4096]{2,1,0:T(8,128)} %bitcast.5, f32[1,4096]{1,0:T(1,128)} %bitcast.6), custom_call_target="tpu_custom_call" | custom-call | tf_op jit(solution)/shard_map/pallas_call | solution.py:798
  50.5 1.6 %shard_map.74 = (f32[1,512]{1,0:T(1,128)}, f32[1,512]{1,0:T(1,128)}, s32[4,512]{1,0:T(4,128)}, f32[32,512]{1,0:T(8,128)}, s32[2,4096]{1,0:T(2,128)}, /*index=5*/f32[1,4096]{1,0:T(1,128)}) custom-call(f32[8,512]{1,0:T(8,128)} %get-tuple-element.15.stat_ref, f32[32,512]{1,0:T(8,128)} %get-tuple-element.16.ld_ref, f32[8,4,512]{2,1,0:T(4,128)} %get-tuple-element.17.samp_ref), custom_call_target="tpu_custom_call" | custom-call | tf_op jit(solution)/shard_map/pallas_call | solution.py:878
